TPU v7x, 128 devices: a whole 4x4x4 slice. The times are simulated.
128 devices in a mesh: tp: 16 (over x_lo, z, core), seq: 8 (over y, x_hi).
Axes of the slice: x: 4 (x_hi: 2, x_lo: 2; x = x_hi * 2 + x_lo), y: 4, z: 4, core: 2. Of those that a mesh axis runs over, the one named last changes fastest.
Arguments:
- residual: bfloat16 [2048, 4096], P('seq'), may hold values from -6 to 6
- mix_gain: float32 [4096], replicated, may hold values from 0.5 to 1.5
- in_proj: bfloat16 [4096, 4096], P(None, 'tp'), may hold values from -0.09375 to 0.09375
- branch_proj: bfloat16 [4096, 4096], P(None, 'tp'), may hold values from -0.09375 to 0.09375
- conv_weight: float32 [4, 4096], P(None, 'tp'), may hold values from -3 to 3
- conv_bias: float32 [4096], P('tp'), may hold values from -1.25 to 1.25
- input_gate: bfloat16 [16, 256, 256], P('tp'), may hold values from -0.375 to 0.375
- input_bias: float32 [4096], P('tp'), may hold values from -3 to 3
- decay_gate: bfloat16 [16, 256, 256], P('tp'), may hold values from -0.375 to 0.375
- decay_bias: float32 [4096], P('tp'), may hold values from -3 to 3
- decay_param: float32 [4096], P('tp'), may hold values from -13 to -2, as said below
- out_proj: bfloat16 [4096, 4096], P('tp'), may hold values from -0.25 to 0.25
- mlp_gain: float32 [4096], replicated, may hold values from 0.5 to 1.5
- gate_proj: bfloat16 [4096, 12288], P('seq', 'tp'), may hold values from -0.09375 to 0.09375
- up_proj: bfloat16 [4096, 12288], P('seq', 'tp'), may hold values from -0.09375 to 0.09375
- down_proj: bfloat16 [12288, 4096], P('tp'), may hold values from -0.078125 to 0.078125
Outputs:
- updated: bfloat16 [2048, 4096], P('seq')
Inputs may be any that keep to these rules, and one draw needn't show every extreme that they name: softplus(decay_param) lies between 0.02 / 2048 and 0.1 for every channel.
All inputs are finite; a program needn't handle non-finite values.
Results may differ from a plain program's by a relative error of at most 0.02.
Values may be sent and summed in bfloat16 or wider, within the bound.
A program may use at most 128 MiB of HBM per device.

v0:
```python
import jax
import jax.numpy as jnp
from jax import lax
from jax.sharding import Mesh
from jax.sharding import PartitionSpec as P

SEQ = ("seq_0", "seq_1")
epsilon = 1e-06


def from_behind(value, axis, steps):
    count = lax.axis_size(axis)
    leading, last = (max(0, -steps), min(count, count - steps))
    return lax.ppermute(value, axis, [(source, source + steps) for source in range(leading, last)])


def whole_of(shard, axes, dim):
    for axis in reversed(axes):
        shard = lax.all_gather(shard, axis, axis=dim, tiled=True)
    return shard


def folded(shard, axis, dim, absorb, state):
    everything = jax.tree.map(lambda a: lax.all_gather(a, axis, axis=dim, tiled=True), shard)
    return absorb(state, everything, jnp.int32(0))


def rms_norm(values, gain):
    wide = values.astype(jnp.float32)
    factor = lax.rsqrt(jnp.mean(wide * wide, axis=-1, keepdims=True) + epsilon)
    return (wide * factor * gain).astype(jnp.bfloat16)


def block_gates(values, weight, bias):
    heads, width = (weight.shape[0], weight.shape[1])
    grouped = values.reshape(values.shape[0], heads, width)
    mixed = jnp.einsum("thi,hij->thj", grouped, weight, preferred_element_type=jnp.float32)
    return jax.nn.sigmoid(mixed.reshape(values.shape[0], heads * width) + bias)


def smooth(inner, tail, conv_weight, conv_bias):
    taps = conv_weight.shape[0]
    length = inner.shape[0]
    padded = jnp.concatenate([tail, inner], axis=0).astype(jnp.float32)
    total = conv_bias + jnp.zeros((length, inner.shape[1]), jnp.float32)
    for offset in range(taps):
        total = total + conv_weight[offset] * padded[taps - 1 - offset : taps - 1 - offset + length]
    return lax.optimization_barrier(total.astype(jnp.bfloat16))


def combine_state(earlier, later):
    return (earlier[0] * later[0], later[0] * earlier[1] + later[1])


def channel_total(partial_value):
    return lax.psum(partial_value.astype(jnp.bfloat16), "tp").astype(jnp.float32)


def on_device(
    residual,
    mix_gain,
    in_proj,
    branch_proj,
    conv_weight,
    conv_bias,
    input_gate,
    input_bias,
    decay_gate,
    decay_bias,
    decay_param,
    out_proj,
    mlp_gain,
    gate_proj,
    up_proj,
    down_proj,
):
    length = residual.shape[0]
    taps = conv_weight.shape[0]
    normed = rms_norm(residual, mix_gain)
    branch = jax.nn.gelu(
        jnp.dot(normed, branch_proj, preferred_element_type=jnp.float32), approximate=True
    )
    inner = jnp.dot(normed, in_proj, preferred_element_type=jnp.float32).astype(jnp.bfloat16)
    tail = from_behind(inner[length - (taps - 1) :], SEQ, 1)
    smoothed = smooth(inner, tail, conv_weight, conv_bias)
    input_rate = block_gates(smoothed, input_gate, input_bias)
    decay_rate = block_gates(smoothed, decay_gate, decay_bias)
    log_decay = -8.0 * decay_rate * jax.nn.softplus(decay_param)
    decay = jnp.exp(log_decay)
    position = lax.axis_index(SEQ)
    first = jnp.logical_and(position == 0, jnp.arange(length) == 0)[:, None]
    scale_in = jnp.where(first, 1.0, jnp.sqrt(-jnp.expm1(2.0 * log_decay)))
    pushed = smoothed.astype(jnp.float32) * input_rate * scale_in
    decays, partial_states = lax.associative_scan(combine_state, (decay, pushed), axis=0)
    end_decay = decays[-1]
    end_state = partial_states[-1]
    summaries = whole_of(jnp.stack([end_decay, end_state])[None], SEQ, 0)

    def fold(index, state):
        moved = summaries[index, 0] * state + summaries[index, 1]
        return jnp.where(index < position, moved, state)

    carried = lax.fori_loop(0, summaries.shape[0], fold, jnp.zeros_like(end_state))
    states = partial_states + decays * carried[None]
    gated = (states * branch).astype(jnp.bfloat16)
    mixed = channel_total(jnp.dot(gated, out_proj, preferred_element_type=jnp.float32))
    middle = lax.optimization_barrier((residual.astype(jnp.float32) + mixed).astype(jnp.bfloat16))
    hidden_in = rms_norm(middle, mlp_gain)
    width = gate_proj.shape[1]
    empty = jnp.zeros((length, width), jnp.float32)

    def add_rows(totals, pieces, start):
        columns = lax.dynamic_slice_in_dim(hidden_in, start, pieces[0].shape[0], 1)
        return (
            totals[0] + jnp.dot(columns, pieces[0], preferred_element_type=jnp.float32),
            totals[1] + jnp.dot(columns, pieces[1], preferred_element_type=jnp.float32),
        )

    gate, up = folded((gate_proj, up_proj), SEQ, 0, add_rows, (empty, empty))
    hidden = (jax.nn.gelu(gate, approximate=True) * up).astype(jnp.bfloat16)
    output = channel_total(jnp.dot(hidden, down_proj, preferred_element_type=jnp.float32))
    return (middle.astype(jnp.float32) + output).astype(jnp.bfloat16)


def solution(mesh):
    split = Mesh(mesh.devices.reshape(mesh.shape["tp"], 4, 2), ("tp", "seq_0", "seq_1"))
    in_specs = (
        P(SEQ, None),
        P(),
        P(None, "tp"),
        P(None, "tp"),
        P(None, "tp"),
        P("tp"),
        P("tp", None, None),
        P("tp"),
        P("tp", None, None),
        P("tp"),
        P("tp"),
        P("tp", None),
        P(),
        P(SEQ, "tp"),
        P(SEQ, "tp"),
        P("tp", None),
    )
    out_specs = P(SEQ, None)
    return jax.shard_map(
        on_device, mesh=split, in_specs=in_specs, out_specs=out_specs, check_vma=False
    )
```

profile of v0, /device:TPU:1, one launch (start us, length us, event | category | flops | bytes accessed | tf_op | source)
XLA Modules:
  0.0 404.2 jit_solution(9161906247059077176)
XLA Ops:
  7.4 2.2 fusion
  9.8 2.5 convolution_convert_fusion.2
  12.3 5.6 %collective-permute-start = (bf16[3,256]{1,0:T(4,128)(2,1)S(1)}, bf16[3,256]{1,0:T(4,128)(2,1)S(1)}, u32[]{:S(2)}, u32[]{:S(2)}) collective-permute-start(bf16[3,256]{1,0:T(4,128)(2,1)S(1)} %slice.348), channel_id=1, source_target_pairs={{0,1},{1,2},{2,3},{3,4},{4,5},{5,6},{6,7},{8,9},{9,10},{10,11},{11... | collective-permute-start | bytes 4616 | tf_op jit(solution)/shard_map/ppermute | solution.py:14
  18.0 0.6 collective-permute-done
  18.8 0.3 fusion.93
  19.1 0.3 fusion.19
  20.9 0.2 slice.330
  21.2 0.2 slice.273
  22.5 0.3 slice-done
  22.9 4.9 %all-gather.1 = f32[2,2,256]{2,1,0:T(2,128)S(1)} all-gather(f32[1,2,256]{2,1,0:T(2,128)S(1)} %maximum_bitcast_fusion), channel_id=2, replica_groups=mesh['tp'=16,'seq_0'=4,'seq_1'=2] {'seq_1'}, dimensions={0}, use_global_device_ids=true | all-gather | bytes 6144 | tf_op jit(solution)/shard_map/all_gather | solution.py:19
  27.9 10.8 %all_gather.13 = f32[8,2,256]{2,1,0:T(2,128)S(1)} all-gather(f32[2,2,256]{2,1,0:T(2,128)S(1)} %all-gather.1), channel_id=1, replica_groups=mesh['tp'=16,'seq_0'=4,'seq_1'=2] {'seq_0'}, dimensions={0}, use_global_device_ids=true | all-gather | bytes 20480 | tf_op jit(solution)/shard_map/all_gather | solution.py:19
  38.6 0.4 while.14
  39.1 6.0 %convolution_convert_fusion = bf16[256,4096]{1,0:T(8,128)(2,1)} fusion(bf16[256,4096]{1,0:T(8,128)(2,1)S(1)} %copy-done, bf16[4096,256]{1,0:T(8,128)(2,1)} %param.21, bf16[256,4096]{1,0:T(8,128)(2,1)} %param.18, f32[4096]{0:T(1024)} %param.19, f32[256]{0:T(256)S(1)} %add_rsqrt_fusion.1, f32[256,256]{1,0:T(8,128)S(1)} %pad.128, f32[256,256]{1,0:T(8,128)S(1)} %pad.129, ...), kind=kOutput, calls=%fused_computation.9 | convolution fusion | flops 1079902208 | bytes 9455616 | tf_op jit(solution)/shard_map/dot_general | solution.py:106
  45.2 0.5 all-gather.5.cloned.1.call-update
  45.7 0.5 all-gather.7.cloned.1.call-update
  46.3 0.2 all-reduce.37.cloned.1.call-start
  46.5 198.7 %all-reduce.35.cloned.1.call-done = bf16[256,4096]{1,0:T(8,128)(2,1)} async-done(((bf16[256,4096]{1,0:T(8,128)(2,1)}), bf16[256,4096]{1,0:T(8,128)(2,1)}) %all-reduce.35.cloned.1.call-update) | async-done | bytes 2097168 | tf_op jit(solution)/shard_map/psum | solution.py:56
  245.2 3.0 fusion.3
  248.2 1.3 copy-done.1
  249.5 0.5 fusion.4
  250.2 5.3 %fusion.29 = f32[256,768]{1,0:T(8,128)S(1)} fusion(bf16[4096,768]{1,0:T(8,128)(2,1)} %all-gather.5.cloned.1.call-done, bf16[256,4096]{1,0:T(8,128)(2,1)} %copy-done.1, f32[4096]{0:T(1024)S(1)} %copy-done.9, f32[256]{0:T(256)S(1)} %add_rsqrt_fusion), kind=kOutput, calls=%fused_computation.43 | convolution fusion | flops 1614807040 | bytes 9192448 | tf_op jit(solution)/shard_map/dot_general | solution.py:115
  255.5 11.3 %convolution_convert_fusion.1 = bf16[256,4096]{1,0:T(8,128)(2,1)} fusion(bf16[768,4096]{1,0:T(8,128)(2,1)} %param.33, bf16[4096,768]{1,0:T(8,128)(2,1)} %all-gather.7.cloned.1.call-done, f32[256,768]{1,0:T(8,128)S(1)} %fusion.29, bf16[256,4096]{1,0:T(8,128)(2,1)} %copy-done.1, f32[4096]{0:T(1024)S(1)} %copy-done.9, f32[256]{0:T(256)S(1)} %add_rsqrt_fusion), kind=kOutput, calls=%fused_computation.10 | convolution fusion | flops 3228434432 | bytes 17581056 | tf_op jit(solution)/shard_map/dot_general | solution.py:121
  266.8 125.6 %all-reduce.37.cloned.1.call-done = bf16[256,4096]{1,0:T(8,128)(2,1)} async-done(((bf16[256,4096]{1,0:T(8,128)(2,1)}), bf16[256,4096]{1,0:T(8,128)(2,1)}) %all-reduce.37.cloned.1.call-update) | async-done | bytes 2097168 | tf_op jit(solution)/shard_map/psum | solution.py:56
  392.4 4.3 %fusion.7 = bf16[256,4096]{1,0:T(8,128)(2,1)} fusion(bf16[256,4096]{1,0:T(8,128)(2,1)} %copy-done.1, bf16[256,4096]{1,0:T(8,128)(2,1)} %all-reduce.37.cloned.1.call-done), kind=kLoop, calls=%fused_computation.18 | loop fusion | flops 4194304 | bytes 6291456 | tf_op jit(solution)/shard_map/convert_element_type | solution.py:122
  (177 shorter events, 3.0 us)
Async XLA Ops:
  7.4 31.7 %copy-start = (bf16[256,4096]{1,0:T(8,128)(2,1)S(1)}, bf16[256,4096]{1,0:T(8,128)(2,1)}, u32[]{:S(2)}) copy-start(bf16[256,4096]{1,0:T(8,128)(2,1)} %param.29) | copy-start | bytes 6291460
  7.4 237.8 %all-reduce.35.cloned.1.call-start = ((), (), s32[]{:S(2)}) async-start(), calls=%async_computation | async-start | bytes 4194304 | tf_op jit(solution)/shard_map/psum | solution.py:56
  7.4 2.4 copy-start.2
  9.7 8.2 %copy-start.4 = (f32[4,256]{1,0:T(4,128)S(1)}, f32[4,256]{1,0:T(4,128)}, u32[]{:S(2)}) copy-start(f32[4,256]{1,0:T(4,128)} %param.22) | copy-start | bytes 12292
  9.7 8.2 %copy-start.5 = (f32[256]{0:T(256)S(1)}, f32[256]{0:T(256)}, u32[]{:S(2)}) copy-start(f32[256]{0:T(256)} %param.28) | copy-start | bytes 3076
  9.7 8.9 %copy-start.6 = (f32[256]{0:T(256)S(1)}, f32[256]{0:T(256)}, u32[]{:S(2)}) copy-start(f32[256]{0:T(256)} %param.23) | copy-start | bytes 3076
  9.8 9.0 %copy-start.7 = (bf16[1,256,256]{2,1,0:T(8,128)(2,1)S(1)}, bf16[1,256,256]{2,1,0:T(8,128)(2,1)}, u32[]{:S(2)}) copy-start(bf16[1,256,256]{2,1,0:T(8,128)(2,1)} %param.26) | copy-start | bytes 393220
  9.8 9.1 %copy-start.10 = (f32[256]{0:T(256)S(1)}, f32[256]{0:T(256)}, u32[]{:S(2)}) copy-start(f32[256]{0:T(256)} %param.27) | copy-start | bytes 3076
  12.2 6.8 %copy-start.8 = (bf16[1,256,256]{2,1,0:T(8,128)(2,1)S(1)}, bf16[1,256,256]{2,1,0:T(8,128)(2,1)}, u32[]{:S(2)}) copy-start(bf16[1,256,256]{2,1,0:T(8,128)(2,1)} %param.24) | copy-start | bytes 393220
  12.3 6.8 %copy-start.11 = (f32[256]{0:T(256)S(1)}, f32[256]{0:T(256)}, u32[]{:S(2)}) copy-start(f32[256]{0:T(256)} %param.25) | copy-start | bytes 3076
  12.3 6.3 %collective-permute-start = (bf16[3,256]{1,0:T(4,128)(2,1)S(1)}, bf16[3,256]{1,0:T(4,128)(2,1)S(1)}, u32[]{:S(2)}, u32[]{:S(2)}) collective-permute-start(bf16[3,256]{1,0:T(4,128)(2,1)S(1)} %slice.348), channel_id=1, source_target_pairs={{0,1},{1,2},{2,3},{3,4},{4,5},{5,6},{6,7},{8,9},{9,10},{10,11},{11... | collective-permute-start | bytes 4616 | tf_op jit(solution)/shard_map/ppermute | solution.py:14
  19.4 2.0 copy-start.3
  22.1 0.7 slice-start
  45.1 204.9 %all-gather.5.cloned.1.call-start = ((), (), s32[]{:S(2)}) async-start(), calls=%async_computation.1 | async-start | bytes 7077888 | tf_op jit(solution)/shard_map/all_gather | solution.py:24
  45.7 209.8 %all-gather.7.cloned.1.call-start = ((), (), s32[]{:S(2)}) async-start(), calls=%async_computation.2 | async-start | bytes 7077888 | tf_op jit(solution)/shard_map/all_gather | solution.py:24
  46.3 346.1 %all-reduce.37.cloned.1.call-start = ((), (), s32[]{:S(2)}) async-start(), calls=%async_computation.3 | async-start | bytes 4194304 | tf_op jit(solution)/shard_map/psum | solution.py:56
  248.2 1.3 copy-start.1
  249.5 0.7 copy-start.9
Sparse Core Ops, SparseCore 0:
  45.2 199.8 all-reduce.34
  266.9 125.4 all-reduce.36
Sparse Core Ops, SparseCore 1:
  47.9 93.9 all-gather.4
  144.0 85.9 all-gather.6
where the time goes:
time: 404 us
  waiting for transfers between devices  326 us (81%)
  matrix products  25.6 us (6%)
  between operations  15.8 us (4%)
  blocking collectives  15.7 us (4%)
  other arithmetic  10.9 us (3%)
  starting transfers between devices  5.91 us (1%)
  local copies, waits for them, and re-layouts  4.04 us (1%)
    psum x2, waiting for transfers between devices, channel_total(): lax.psum(partial_value.astype(jnp.bfloat16), 'tp').astype(jnp.float32)  324 us
    all_gather x2, blocking collectives, whole_of(): shard = lax.all_gather(shard, axis, axis=dim, tiled=True)  15.7 us
    dot_general x1, matrix products, on_device(): jnp.dot(hidden, down_proj, preferred_element_type=jnp.float32)  11.3 us
  transfers between devices with their start and end apart: 5, of which 3 were waited for; matrix products, arithmetic and copies ran while one was open for 2% of the time, Pallas kernels for 0%

commit v1 on v0

--- a/solution.py
+++ b/solution.py
@@ -6,6 +6,12 @@
 
 SEQ = ("seq_0", "seq_1")
 epsilon = 1e-06
+
+
+def gather_and_add(shard, mesh_axis):
+    blocks = lax.all_gather(shard, mesh_axis, axis=0, tiled=False)
+    total = blocks.sum(axis=0)
+    return total
 
 
 def from_behind(value, axis, steps):
@@ -53,7 +59,7 @@
 
 
 def channel_total(partial_value):
-    return lax.psum(partial_value.astype(jnp.bfloat16), "tp").astype(jnp.float32)
+    return gather_and_add(partial_value.astype(jnp.bfloat16), "tp").astype(jnp.float32)
 
 
 def on_device(

time: 404 us -> 605 us (1.50)
  waiting for transfers between devices: 326 us -> 505 us
  other arithmetic: 10.9 us -> 37.3 us
    all_gather x0 -> x2, waiting for transfers between devices: none -> 345 us  [gather_and_add(): blocks = lax.all_gather(shard, mesh_axis, axis=0, tiled=False)]
    psum x2 -> x0, waiting for transfers between devices: 324 us -> none  [channel_total(): lax.psum(partial_value.astype(jnp.bfloat16), 'tp').astype(jnp.float32)]
    all_gather x2, waiting for transfers between devices: 0.05 us -> 158 us  [folded(): lax.all_gather(a, axis, axis=dim, tiled=True)]
    reduce_sum x0 -> x2, other arithmetic: none -> 26.1 us  [gather_and_add(): total = blocks.sum(axis=0)]
  transfers between devices with their start and end apart: 5 -> 5, of which waited for: 3 -> 5; matrix products, arithmetic and copies ran while one was open for 2% -> 4% of each run, Pallas kernels for 0% -> 0%
where the time goes in v1:
time: 605 us
  waiting for transfers between devices  505 us (83%)
  other arithmetic  37.3 us (6%)
  matrix products  24.3 us (4%)
  blocking collectives  15.7 us (3%)
  between operations  14 us (2%)
    all_gather x2, waiting for transfers between devices, gather_and_add(): blocks = lax.all_gather(shard, mesh_axis, axis=0, tiled=False)  345 us
    all_gather x2, waiting for transfers between devices, folded(): lax.all_gather(a, axis, axis=dim, tiled=True)  158 us
    reduce_sum x2, other arithmetic, gather_and_add(): total = blocks.sum(axis=0)  26.1 us
    all_gather x2, blocking collectives, whole_of(): shard = lax.all_gather(shard, axis, axis=dim, tiled=True)  15.7 us
  transfers between devices with their start and end apart: 5, of which 5 were waited for; matrix products, arithmetic and copies ran while one was open for 4% of the time, Pallas kernels for 0%

profile of v1, /device:TPU:1, one launch (start us, length us, event | category | flops | bytes accessed | tf_op | source)
XLA Modules:
  0.0 605.2 jit_solution(12152965135691595950)
XLA Ops:
  6.5 2.2 fusion
  8.9 2.5 convolution_convert_fusion.2
  11.4 5.6 collective-permute-start
  17.2 0.6 collective-permute-done
  18.0 0.3 fusion.93
  18.3 0.3 fusion.19
  21.7 0.3 slice-done
  22.1 4.9 all-gather.3
  27.0 10.8 %all_gather.25 = f32[8,2,256]{2,1,0:T(2,128)S(1)} all-gather(f32[2,2,256]{2,1,0:T(2,128)S(1)} %all-gather.3), channel_id=1, replica_groups=mesh['tp'=16,'seq_0'=4,'seq_1'=2] {'seq_0'}, dimensions={0}, use_global_device_ids=true | all-gather | bytes 20480 | tf_op jit(solution)/shard_map/all_gather | solution.py:25
  37.8 0.4 while.14
  38.2 6.0 convolution_convert_fusion
  44.3 0.7 all-gather.9.cloned.1.call-update
  45.1 0.7 all-gather.11.cloned.1.call-update
  46.0 175.4 %all-gather.13.cloned.1.call-done = bf16[4096,4096]{1,0:T(8,128)(2,1)} async-done(((bf16[256,4096]{1,0:T(8,128)(2,1)}), bf16[4096,4096]{1,0:T(8,128)(2,1)}) %all-gather.13.cloned.1.call-update) | async-done | bytes 33554448 | tf_op jit(solution)/shard_map/all_gather | solution.py:12
  221.4 13.0 %reduce_sum.43 = bf16[256,4096]{1,0:T(8,128)(2,1)} reduce(bf16[16,256,4096]{2,1,0:T(8,128)(2,1)} %bitcast.30, bf16[]{:T(256)} %constant.65.clone.1), dimensions={0}, to_apply=%region_3.4 | reduce | flops 15728640 | bytes 35651584 | tf_op jit(solution)/shard_map/reduce_sum | solution.py:13
  234.4 3.4 fusion.3
  237.8 0.5 fusion.4
  238.3 73.8 %all-gather.9.cloned.1.call-done = bf16[4096,768]{1,0:T(8,128)(2,1)} async-done(((bf16[512,768]{1,0:T(8,128)(2,1)}), bf16[4096,768]{1,0:T(8,128)(2,1)}) %all-gather.9.cloned.1.call-update) | async-done | bytes 6291472 | tf_op jit(solution)/shard_map/all_gather | solution.py:30
  312.1 4.6 fusion.29
  316.7 84.1 %all-gather.11.cloned.1.call-done = bf16[4096,768]{1,0:T(8,128)(2,1)} async-done(((bf16[512,768]{1,0:T(8,128)(2,1)}), bf16[4096,768]{1,0:T(8,128)(2,1)}) %all-gather.11.cloned.1.call-update) | async-done | bytes 6291472 | tf_op jit(solution)/shard_map/all_gather | solution.py:30
  400.8 10.6 %convolution_convert_fusion.1 = bf16[256,4096]{1,0:T(8,128)(2,1)} fusion(bf16[768,4096]{1,0:T(8,128)(2,1)} %param.33, bf16[4096,768]{1,0:T(8,128)(2,1)} %all-gather.11.cloned.1.call-done, f32[256,768]{1,0:T(8,128)S(1)} %fusion.29, bf16[256,4096]{1,0:T(8,128)(2,1)S(1)} %fusion.3, f32[4096]{0:T(1024)S(1)} %copy-done.10, f32[256]{0:T(256)S(1)} %add_rsqrt_fusion), kind=kOutput, calls=%fused_computation.10 | convolution fusion | flops 3228434432 | bytes 17581056 | tf_op jit(solution)/shard_map/dot_general | solution.py:127
  411.4 169.8 %all-gather.15.cloned.1.call-done = bf16[4096,4096]{1,0:T(8,128)(2,1)} async-done(((bf16[256,4096]{1,0:T(8,128)(2,1)}), bf16[4096,4096]{1,0:T(8,128)(2,1)}) %all-gather.15.cloned.1.call-update) | async-done | bytes 33554448 | tf_op jit(solution)/shard_map/all_gather | solution.py:12
  581.2 13.1 %reduce_sum.45 = bf16[256,4096]{1,0:T(8,128)(2,1)} reduce(bf16[16,256,4096]{2,1,0:T(8,128)(2,1)} %bitcast.31, bf16[]{:T(256)} %constant.65.clone.1), dimensions={0}, to_apply=%region_5.6 | reduce | flops 15728640 | bytes 35651584 | tf_op jit(solution)/shard_map/reduce_sum | solution.py:13
  594.3 4.3 fusion.7
  (181 shorter events, 3.4 us)
Async XLA Ops:
  6.5 31.7 %copy-start = (bf16[256,4096]{1,0:T(8,128)(2,1)S(1)}, bf16[256,4096]{1,0:T(8,128)(2,1)}, u32[]{:S(2)}) copy-start(bf16[256,4096]{1,0:T(8,128)(2,1)} %param.29) | copy-start | bytes 6291460
  6.5 214.9 %all-gather.13.cloned.1.call-start = ((), (), s32[]{:S(2)}) async-start(), calls=%async_computation.2 | async-start | bytes 35651584 | tf_op jit(solution)/shard_map/all_gather | solution.py:12
  6.5 2.4 copy-start.3
  8.9 8.2 %copy-start.5 = (f32[4,256]{1,0:T(4,128)S(1)}, f32[4,256]{1,0:T(4,128)}, u32[]{:S(2)}) copy-start(f32[4,256]{1,0:T(4,128)} %param.22) | copy-start | bytes 12292
  8.9 8.2 %copy-start.6 = (f32[256]{0:T(256)S(1)}, f32[256]{0:T(256)}, u32[]{:S(2)}) copy-start(f32[256]{0:T(256)} %param.28) | copy-start | bytes 3076
  8.9 8.9 %copy-start.7 = (f32[256]{0:T(256)S(1)}, f32[256]{0:T(256)}, u32[]{:S(2)}) copy-start(f32[256]{0:T(256)} %param.23) | copy-start | bytes 3076
  8.9 9.1 %copy-start.8 = (bf16[1,256,256]{2,1,0:T(8,128)(2,1)S(1)}, bf16[1,256,256]{2,1,0:T(8,128)(2,1)}, u32[]{:S(2)}) copy-start(bf16[1,256,256]{2,1,0:T(8,128)(2,1)} %param.26) | copy-start | bytes 393220
  8.9 9.1 %copy-start.11 = (f32[256]{0:T(256)S(1)}, f32[256]{0:T(256)}, u32[]{:S(2)}) copy-start(f32[256]{0:T(256)} %param.27) | copy-start | bytes 3076
  11.4 6.9 %copy-start.9 = (bf16[1,256,256]{2,1,0:T(8,128)(2,1)S(1)}, bf16[1,256,256]{2,1,0:T(8,128)(2,1)}, u32[]{:S(2)}) copy-start(bf16[1,256,256]{2,1,0:T(8,128)(2,1)} %param.24) | copy-start | bytes 393220
  11.4 6.9 %copy-start.12 = (f32[256]{0:T(256)S(1)}, f32[256]{0:T(256)}, u32[]{:S(2)}) copy-start(f32[256]{0:T(256)} %param.25) | copy-start | bytes 3076
  11.4 6.3 %collective-permute-start = (bf16[3,256]{1,0:T(4,128)(2,1)S(1)}, bf16[3,256]{1,0:T(4,128)(2,1)S(1)}, u32[]{:S(2)}, u32[]{:S(2)}) collective-permute-start(bf16[3,256]{1,0:T(4,128)(2,1)S(1)} %slice.348), channel_id=1, source_target_pairs={{0,1},{1,2},{2,3},{3,4},{4,5},{5,6},{6,7},{8,9},{9,10},{10,11},{11... | collective-permute-start | bytes 4616 | tf_op jit(solution)/shard_map/ppermute | solution.py:20
  18.6 2.0 copy-start.4
  21.3 0.7 slice-start
  44.3 267.8 %all-gather.9.cloned.1.call-start = ((), (), s32[]{:S(2)}) async-start(), calls=%async_computation | async-start | bytes 7077888 | tf_op jit(solution)/shard_map/all_gather | solution.py:30
  45.0 355.8 %all-gather.11.cloned.1.call-start = ((), (), s32[]{:S(2)}) async-start(), calls=%async_computation.1 | async-start | bytes 7077888 | tf_op jit(solution)/shard_map/all_gather | solution.py:30
  45.8 535.5 %all-gather.15.cloned.1.call-start = ((), (), s32[]{:S(2)}) async-start(), calls=%async_computation.3 | async-start | bytes 35651584 | tf_op jit(solution)/shard_map/all_gather | solution.py:12
  237.8 163.0 %copy-start.2 = (bf16[256,4096]{1,0:T(8,128)(2,1)}, bf16[256,4096]{1,0:T(8,128)(2,1)S(1)}, u32[]{:S(2)}) copy-start(bf16[256,4096]{1,0:T(8,128)(2,1)S(1)} %fusion.3) | copy-start | bytes 6291460
  237.8 74.3 %copy-start.10 = (f32[4096]{0:T(1024)S(1)}, f32[4096]{0:T(1024)}, u32[]{:S(2)}) copy-start(f32[4096]{0:T(1024)} %param.30) | copy-start | bytes 49156
  581.2 17.4 %copy-start.1 = (bf16[256,4096]{1,0:T(8,128)(2,1)S(1)}, bf16[256,4096]{1,0:T(8,128)(2,1)}, u32[]{:S(2)}) copy-start(bf16[256,4096]{1,0:T(8,128)(2,1)} %param.29) | copy-start | bytes 6291460
Sparse Core Ops, SparseCore 0:
  44.4 176.9 all-gather.12
  223.7 88.2 all-gather.8
  314.4 86.3 all-gather.10
  411.5 169.6 all-gather.14
